TPU v7x, 32 devices: a whole 2x2x4 slice. The times are simulated.
32 devices in a mesh: gx: 8 (over z, core), gy: 4 (over y, x).
Axes of the slice: x: 2, y: 2, z: 4, core: 2. Of those that a mesh axis runs over, the one named last changes fastest.
Arguments:
- earlier_heat_field: float32 [6, 1024, 512], P(None, 'gx', 'gy'), may hold values from -6 to 6
- substance_per_voxel: int32 [6, 1024, 512], P(None, 'gx', 'gy'), may hold values from 0 to 7
- patch_wattage_category: int32 [64, 32], P('gx', 'gy'), may hold values from 0 to 63
- planar_coupling: float32 [8], replicated, may hold values from 0.3 to 3
- vertical_coupling_per_substance: float32 [8], replicated, may hold values from 0.05 to 0.5
- heat_mass_ratio: float32 [8], replicated, may hold values from 2e-05 to 0.0002
- wattage_per_category: float32 [64], replicated, may hold values from 2e-06 to 2e-05
Outputs:
- temperature: float32 [6, 1024, 512], P(None, 'gx', 'gy')
All inputs are finite; a program needn't handle non-finite values.
Results may differ from a plain program's by a relative error of at most 0.0003.
Values sent between devices are 32-bit elements; how exact they have to be, the bound alone decides.
A program may use at most 192 MiB of HBM per device.

v0:
```python
import jax
import jax.numpy as jnp
from jax import lax
from jax.sharding import PartitionSpec as P

TILE = 16
LEVELS = 6
SWEEPS = 2
COARSE_ITERS = 12


def extended(block, sides, width):
    for axis, dim in sides:
        count = lax.axis_size(axis)
        forward = [(i, i + 1) for i in range(count - 1)]
        backward = [(target, source) for source, target in forward]
        low = lax.ppermute(
            lax.slice_in_dim(block, block.shape[dim] - width, None, axis=dim), axis, forward
        )
        high = lax.ppermute(lax.slice_in_dim(block, 0, width, axis=dim), axis, backward)
        block = jnp.concatenate([low, block, high], axis=dim)
    return block


def previous(values, dimension):
    widths = [(0, 0)] * values.ndim
    widths[dimension] = (1, 0)
    return lax.slice_in_dim(jnp.pad(values, widths), 0, values.shape[dimension], axis=dimension)


def following(values, dimension):
    widths = [(0, 0)] * values.ndim
    widths[dimension] = (0, 1)
    return lax.slice_in_dim(jnp.pad(values, widths), 1, values.shape[dimension] + 1, axis=dimension)


def stencil(lateral, vertical, capacity_diagonal, inside, factor):
    row_before = factor * 0.5 * (lateral + previous(lateral, 1))
    row_after = factor * 0.5 * (lateral + following(lateral, 1))
    col_before = factor * 0.5 * (lateral + previous(lateral, 2))
    col_after = factor * 0.5 * (lateral + following(lateral, 2))
    faces = 0.5 * (vertical[1:] + vertical[:-1])
    no_face = jnp.zeros_like(vertical[:1])
    layer_below = jnp.concatenate([no_face, faces], 0)
    layer_above = jnp.concatenate([faces, no_face], 0)
    diagonal = (
        capacity_diagonal
        + row_before
        + row_after
        + col_before
        + col_after
        + layer_below
        + layer_above
    )
    diagonal = jnp.where(inside > 0, diagonal, 1.0)
    return (row_before, row_after, col_before, col_after, layer_below, layer_above, diagonal)


def coupled(values, weights):
    summed = weights[0] * previous(values, 1) + weights[1] * following(values, 1)
    summed = summed + weights[2] * previous(values, 2) + weights[3] * following(values, 2)
    return summed + weights[4] * previous(values, 0) + weights[5] * following(values, 0)


def parity(extent):
    summed = lax.broadcasted_iota(jnp.int32, extent, 0) + lax.broadcasted_iota(jnp.int32, extent, 1)
    return (summed + lax.broadcasted_iota(jnp.int32, extent, 2)) % 2


def restrict(values):
    layers, height, breadth = values.shape
    blocks = values.reshape(layers, height // 2, 2, breadth // 2, 2)
    return (
        blocks[:, :, 0, :, 0]
        + blocks[:, :, 1, :, 0]
        + blocks[:, :, 0, :, 1]
        + blocks[:, :, 1, :, 1]
    ) * 0.25


def prolong(values):
    return jnp.repeat(jnp.repeat(values, 2, axis=1), 2, axis=2)


def lookup(labels, entries):
    summed = jnp.zeros(labels.shape, entries.dtype)
    for number in range(entries.shape[0]):
        summed = summed + jnp.where(labels == number, entries[number], 0.0)
    return summed


def conjugate(source_vector, weights):
    solution = jnp.zeros_like(source_vector)
    residue = source_vector
    precond = residue / weights[6]
    search = precond
    inner = jnp.sum(residue * precond)
    for step_index in range(COARSE_ITERS):
        image = weights[6] * search - coupled(search, weights)
        alpha_step = inner / jnp.sum(search * image)
        solution = solution + alpha_step * search
        residue = residue - alpha_step * image
        precond = residue / weights[6]
        inner_next = jnp.sum(residue * precond)
        search = precond + inner_next / inner * search
        inner = inner_next
    return solution


def update(beside_all, rhs_pad, weights, colours, inside, colour, margin):
    extent = beside_all.shape
    row_index = lax.broadcasted_iota(jnp.int32, extent, 1)
    col_index = lax.broadcasted_iota(jnp.int32, extent, 2)
    region = (row_index >= margin) & (row_index < extent[1] - margin)
    region = region & (col_index >= margin) & (col_index < extent[2] - margin)
    candidate = (rhs_pad + coupled(beside_all, weights)) / weights[6]
    chosen = (colours == colour) & region & (inside > 0)
    return jnp.where(chosen, candidate, beside_all)


def smooth(present_guess, rhs_pad, level_data):
    wide, narrow, colours_wide, inside_wide = level_data
    for sweep_index in range(SWEEPS):
        beside_all = extended(present_guess, (("gx", 1), ("gy", 2)), 2)
        beside_all = update(beside_all, rhs_pad, wide, colours_wide, inside_wide, 0, 1)
        beside_all = update(beside_all, rhs_pad, wide, colours_wide, inside_wide, 1, 2)
        present_guess = beside_all[:, 2:-2, 2:-2]
    return present_guess


def on_device(
    earlier_heat_field,
    substance_per_voxel,
    patch_wattage_category,
    planar_coupling,
    vertical_coupling_per_substance,
    heat_mass_ratio,
    wattage_per_category,
):
    lateral = lookup(substance_per_voxel, planar_coupling)
    vertical = lookup(substance_per_voxel, vertical_coupling_per_substance)
    capacity_diagonal = lookup(substance_per_voxel, heat_mass_ratio)
    heat = jnp.repeat(
        jnp.repeat(lookup(patch_wattage_category, wattage_per_category), TILE, axis=0), TILE, axis=1
    )
    source_vector = capacity_diagonal * earlier_heat_field
    source_vector = jnp.concatenate([source_vector[:1] + heat[None], source_vector[1:]], 0)
    coefficients = [(lateral, vertical, capacity_diagonal)]
    for level_index in range(LEVELS):
        last = coefficients[-1]
        coefficients.append((restrict(last[0]), restrict(last[1]), restrict(last[2])))
    coarse_lateral, coarse_vertical, coarse_storage = coefficients[LEVELS]
    stencils = []
    for level_index in range(LEVELS):
        level_coef = coefficients[level_index]
        padded = (
            extended(level_coef[0], (("gx", 1), ("gy", 2)), 2),
            extended(level_coef[1], (("gx", 1), ("gy", 2)), 2),
            extended(level_coef[2], (("gx", 1), ("gy", 2)), 2),
            extended(jnp.ones_like(level_coef[0]), (("gx", 1), ("gy", 2)), 2),
        )
        wide = stencil(padded[0], padded[1], padded[2], padded[3], 0.25**level_index)
        narrow = tuple((member[:, 1:-1, 1:-1] for member in wide))
        stencils.append((wide, narrow, parity(padded[0].shape), padded[3]))
    present_guess = earlier_heat_field
    saved = []
    for level_index in range(LEVELS):
        narrow = stencils[level_index][1]
        rhs_pad = extended(source_vector, (("gx", 1), ("gy", 2)), 2)
        present_guess = smooth(present_guess, rhs_pad, stencils[level_index])
        beside_all = extended(present_guess, (("gx", 1), ("gy", 2)), 1)
        residual = (
            source_vector - (narrow[6] * beside_all - coupled(beside_all, narrow))[:, 1:-1, 1:-1]
        )
        saved.append((present_guess, rhs_pad))
        source_vector = restrict(residual)
        present_guess = jnp.zeros_like(source_vector)
    whole = (
        lax.all_gather(source_vector, "gx", axis=1, tiled=True),
        lax.all_gather(coarse_lateral, "gx", axis=1, tiled=True),
        lax.all_gather(coarse_vertical, "gx", axis=1, tiled=True),
        lax.all_gather(coarse_storage, "gx", axis=1, tiled=True),
    )
    whole = (
        lax.all_gather(whole[0], "gy", axis=2, tiled=True),
        lax.all_gather(whole[1], "gy", axis=2, tiled=True),
        lax.all_gather(whole[2], "gy", axis=2, tiled=True),
        lax.all_gather(whole[3], "gy", axis=2, tiled=True),
    )
    whole_rhs = whole[0]
    whole_coef = (whole[1], whole[2], whole[3])
    coarse_weights = stencil(
        whole_coef[0], whole_coef[1], whole_coef[2], jnp.ones_like(whole_rhs), 0.25**LEVELS
    )
    solution = conjugate(whole_rhs, coarse_weights)
    start_row = lax.axis_index("gx") * source_vector.shape[1]
    start_col = lax.axis_index("gy") * source_vector.shape[2]
    correction = lax.dynamic_slice(
        solution, (jnp.int32(0), start_row, start_col), source_vector.shape
    )
    for level_index in reversed(range(LEVELS)):
        present_guess, rhs_pad = saved[level_index]
        present_guess = smooth(present_guess + prolong(correction), rhs_pad, stencils[level_index])
        correction = present_guess
    return correction


def solution(mesh):
    placed = (P(None, "gx", "gy"), P(None, "gx", "gy"), P("gx", "gy"), P(), P(), P(), P())
    return jax.shard_map(
        on_device, mesh=mesh, in_specs=placed, out_specs=P(None, "gx", "gy"), check_vma=False
    )
```

profile of v0, /device:TPU:1, one launch (start us, length us, event | category | flops | bytes accessed | tf_op | source)
XLA Modules:
  0.0 1529.4 jit_solution(2888406218585985499)
XLA Ops:
  12.9 6.4 fusion.553
  19.3 5.2 select_add_fusion.1
  24.5 7.6 copy.1151
  32.1 12.5 fusion.554
  65.0 5.2 fusion.558
  82.5 7.6 copy.1164
  90.1 12.5 fusion.555
  122.9 5.4 fusion.559
  144.4 5.3 select_add_fusion
  149.7 7.6 copy.1159
  173.4 12.5 fusion.557
  206.2 5.3 fusion.561
  222.7 11.7 all-gather.6
  234.5 6.2 all-gather.7
  241.3 39.8 %select_add_fusion.3 = f32[8,8]{1,0:T(8,128)S(1)} fusion(s32[8,8]{1,0:T(8,128)S(1)} %copy-done.288, f32[]{:T(128)} %bitcast.71, f32[]{:T(128)} %bitcast.70, f32[]{:T(128)} %bitcast.69, f32[]{:T(128)} %bitcast.68, f32[]{:T(128)} %bitcast.67, f32[]{:T(128)} %bitcast.66, f32[]{:T(128)} %bitcast.65, f32[]{:T(128)} %bitcast.64, f32[]{:T(128)} %bitcast.63, ...), kind=kLoop, calls=%fused_computation.1216 | loop fusion | flops 12224 | bytes 768 | tf_op jit(solution)/shard_map/add | solution.py:88
  289.8 14.8 all-gather.4
  304.7 6.1 all-gather.5
  311.4 14.9 all-gather.2
  326.4 6.1 all-gather.3
  559.1 5.6 collective-permute-start.42
  566.2 6.5 fusion.4
  576.6 5.6 collective-permute-start.24
  613.3 5.9 collective-permute-start.32
  643.9 8.5 copy.1146
  652.4 12.5 fusion.556
  664.9 5.6 copy.1277
  670.6 5.6 copy.1278
  676.2 5.6 copy.1279
  681.8 5.6 copy.1280
  688.7 5.6 collective-permute-start.36
  726.8 6.0 collective-permute-start.56
  756.7 6.4 collective-permute-done.59
  765.5 4.9 collective-permute-start.64
  787.7 5.1 collective-permute-done.67
  797.8 5.5 fusion.560
  812.1 5.5 collective-permute-start.68
  847.9 5.3 collective-permute-start.88
  882.5 5.7 collective-permute-start.96
  892.9 5.0 collective-permute-start.118
  924.7 5.6 collective-permute-start.100
  970.3 6.2 collective-permute-start.120
  1003.2 5.0 collective-permute-start.130
  1009.9 5.8 collective-permute-start.126
  1022.2 4.9 collective-permute-start.182
  1051.7 5.4 collective-permute-start.152
  1116.4 5.3 collective-permute-start.184
  1155.3 12.9 all-gather
  1169.6 6.8 all-gather.1
  (1624 shorter events, 1120.0 us)
Async XLA Ops:
  0.8 531.4 %collective-permute-start = (f32[6,2,128]{1,2,0:T(8,128)}, f32[6,2,128]{1,2,0:T(8,128)}, u32[]{:S(2)}, u32[]{:S(2)}) collective-permute-start(f32[6,2,128]{1,2,0:T(8,128)} %broadcast.1280), channel_id=1, source_target_pairs={{0,4},{4,8},{8,12},{12,16},{16,20},{20,24},{24,28},{1,5},{5,9},{9,... | collective-permute-start | bytes 18440 | tf_op jit(solution)/shard_map/ppermute | solution.py:17
  5.4 531.1 %collective-permute-start.1 = (f32[6,2,128]{1,2,0:T(8,128)}, f32[6,2,128]{1,2,0:T(8,128)}, u32[]{:S(2)}, u32[]{:S(2)}) collective-permute-start(f32[6,2,128]{1,2,0:T(8,128)} %broadcast.1280), channel_id=1, source_target_pairs={{4,0},{8,4},{12,8},{16,12},{20,16},{24,20},{28,24},{5,1},{9,5},{13... | collective-permute-start | bytes 18440 | tf_op jit(solution)/shard_map/ppermute | solution.py:20
  76.7 257.5 %collective-permute-start.168 = (f32[6,2,4]{0,2,1:T(4,128)}, f32[6,2,4]{0,2,1:T(4,128)}, u32[]{:S(2)}, u32[]{:S(2)}) collective-permute-start(f32[6,2,4]{0,2,1:T(4,128)} %get-tuple-element.495), channel_id=1, source_target_pairs={{0,4},{4,8},{8,12},{12,16},{16,20},{20,24},{24,28},{1,5},{5,9},{9,... | collective-permute-start | bytes 584 | tf_op jit(solution)/shard_map/ppermute | solution.py:17
  80.4 258.0 %collective-permute-start.169 = (f32[6,2,4]{0,2,1:T(4,128)S(1)}, f32[6,2,4]{0,2,1:T(4,128)}, u32[]{:S(2)}, u32[]{:S(2)}) collective-permute-start(f32[6,2,4]{0,2,1:T(4,128)S(1)} %get-tuple-element.496), channel_id=1, source_target_pairs={{4,0},{8,4},{12,8},{16,12},{20,16},{24,20},{28,24},{5,1},{9,5},{13... | collective-permute-start | bytes 584 | tf_op jit(solution)/shard_map/ppermute | solution.py:20
  136.0 205.7 %collective-permute-start.180 = (f32[6,2,4]{0,2,1:T(4,128)}, f32[6,2,4]{0,2,1:T(4,128)S(1)}, u32[]{:S(2)}, u32[]{:S(2)}) collective-permute-start(f32[6,2,4]{0,2,1:T(4,128)} %get-tuple-element.497), channel_id=1, source_target_pairs={{0,4},{4,8},{8,12},{12,16},{16,20},{20,24},{24,28},{1,5},{5,9},{9,... | collective-permute-start | bytes 584 | tf_op jit(solution)/shard_map/ppermute | solution.py:17
  388.0 15.9 %collective-permute-start.104 = (f32[6,2,16]{2,1,0:T(2,128)S(1)}, f32[6,2,16]{2,1,0:T(2,128)S(1)}, u32[]{:S(2)}, u32[]{:S(2)}) collective-permute-start(f32[6,2,16]{2,1,0:T(2,128)S(1)} %get-tuple-element.411), channel_id=1, source_target_pairs={{0,4},{4,8},{8,12},{12,16},{16,20},{20,24},{24,28},{1,5},{5,9},{9,... | collective-permute-start | bytes 2312 | tf_op jit(solution)/shard_map/ppermute | solution.py:17
  451.2 17.2 %collective-permute-start.40 = (f32[6,2,64]{2,1,0:T(2,128)}, f32[6,2,64]{2,1,0:T(2,128)S(1)}, u32[]{:S(2)}, u32[]{:S(2)}) collective-permute-start(f32[6,2,64]{2,1,0:T(2,128)} %get-tuple-element.265), channel_id=1, source_target_pairs={{0,4},{4,8},{8,12},{12,16},{16,20},{20,24},{24,28},{1,5},{5,9},{9,... | collective-permute-start | bytes 9224 | tf_op jit(solution)/shard_map/ppermute | solution.py:17
  522.3 23.0 %collective-permute-start.10 = (f32[6,132,2]{1,2,0:T(2,128)S(1)}, f32[6,132,2]{1,2,0:T(2,128)S(1)}, u32[]{:S(2)}, u32[]{:S(2)}) collective-permute-start(f32[6,132,2]{1,2,0:T(2,128)S(1)} %get-tuple-element.173), channel_id=1, source_target_pairs={{0,1},{1,2},{2,3},{4,5},{5,6},{6,7},{8,9},{9,10},{10,11},{12,13},{... | collective-permute-start | bytes 19016 | tf_op jit(solution)/shard_map/ppermute | solution.py:17
  526.4 23.3 %collective-permute-start.11 = (f32[6,132,2]{1,2,0:T(2,128)S(1)}, f32[6,132,2]{1,2,0:T(2,128)S(1)}, u32[]{:S(2)}, u32[]{:S(2)}) collective-permute-start(f32[6,132,2]{1,2,0:T(2,128)S(1)} %get-tuple-element.174), channel_id=1, source_target_pairs={{1,0},{2,1},{3,2},{5,4},{6,5},{7,6},{9,8},{10,9},{11,10},{13,12},{... | collective-permute-start | bytes 19016 | tf_op jit(solution)/shard_map/ppermute | solution.py:20
  528.0 23.4 %collective-permute-start.6 = (f32[6,132,2]{1,2,0:T(2,128)S(1)}, f32[6,132,2]{1,2,0:T(2,128)S(1)}, u32[]{:S(2)}, u32[]{:S(2)}) collective-permute-start(f32[6,132,2]{1,2,0:T(2,128)S(1)} %get-tuple-element.177), channel_id=1, source_target_pairs={{0,1},{1,2},{2,3},{4,5},{5,6},{6,7},{8,9},{9,10},{10,11},{12,13},{... | collective-permute-start | bytes 19016 | tf_op jit(solution)/shard_map/ppermute | solution.py:17
  538.7 20.3 %collective-permute-start.7 = (f32[6,132,2]{1,2,0:T(2,128)S(1)}, f32[6,132,2]{1,2,0:T(2,128)S(1)}, u32[]{:S(2)}, u32[]{:S(2)}) collective-permute-start(f32[6,132,2]{1,2,0:T(2,128)S(1)} %get-tuple-element.178), channel_id=1, source_target_pairs={{1,0},{2,1},{3,2},{5,4},{6,5},{7,6},{9,8},{10,9},{11,10},{13,12},{... | collective-permute-start | bytes 19016 | tf_op jit(solution)/shard_map/ppermute | solution.py:20
  541.2 23.4 %collective-permute-start.22 = (f32[6,132,2]{1,2,0:T(2,128)S(1)}, f32[6,132,2]{1,2,0:T(2,128)S(1)}, u32[]{:S(2)}, u32[]{:S(2)}) collective-permute-start(f32[6,132,2]{1,2,0:T(2,128)S(1)} %get-tuple-element.175), channel_id=1, source_target_pairs={{0,1},{1,2},{2,3},{4,5},{5,6},{6,7},{8,9},{9,10},{10,11},{12,13},{... | collective-permute-start | bytes 19016 | tf_op jit(solution)/shard_map/ppermute | solution.py:17
  559.1 145.4 %collective-permute-start.42 = (f32[6,68,2]{2,1,0:T(8,128)}, f32[6,68,2]{2,1,0:T(8,128)}, u32[]{:S(2)}, u32[]{:S(2)}) collective-permute-start(f32[6,68,2]{2,1,0:T(8,128)} %get-tuple-element.253), channel_id=1, source_target_pairs={{0,1},{1,2},{2,3},{4,5},{5,6},{6,7},{8,9},{9,10},{10,11},{12,13},{... | collective-permute-start | bytes 9800 | tf_op jit(solution)/shard_map/ppermute | solution.py:17
  564.7 38.7 %collective-permute-start.51 = (f32[6,68,2]{2,1,0:T(8,128)}, f32[6,68,2]{2,1,0:T(8,128)}, u32[]{:S(2)}, u32[]{:S(2)}) collective-permute-start(f32[6,68,2]{2,1,0:T(8,128)} %get-tuple-element.260), channel_id=1, source_target_pairs={{1,0},{2,1},{3,2},{5,4},{6,5},{7,6},{9,8},{10,9},{11,10},{13,12},{... | collective-permute-start | bytes 9800 | tf_op jit(solution)/shard_map/ppermute | solution.py:20
  576.6 15.9 %collective-permute-start.24 = (f32[6,2,128]{1,2,0:T(8,128)}, f32[6,2,128]{1,2,0:T(8,128)}, u32[]{:S(2)}, u32[]{:S(2)}) collective-permute-start(f32[6,2,128]{1,2,0:T(8,128)} %get-tuple-element.197), channel_id=1, source_target_pairs={{0,4},{4,8},{8,12},{12,16},{16,20},{20,24},{24,28},{1,5},{5,9},{9,... | collective-permute-start | bytes 18440 | tf_op jit(solution)/shard_map/ppermute | solution.py:17
  592.5 28.6 %collective-permute-start.46 = (f32[6,68,2]{1,2,0:T(2,128)S(1)}, f32[6,68,2]{1,2,0:T(2,128)S(1)}, u32[]{:S(2)}, u32[]{:S(2)}) collective-permute-start(f32[6,68,2]{1,2,0:T(2,128)S(1)} %copy-done.287), channel_id=1, source_target_pairs={{0,1},{1,2},{2,3},{4,5},{5,6},{6,7},{8,9},{9,10},{10,11},{12,13},{... | collective-permute-start | bytes 9800 | tf_op jit(solution)/shard_map/ppermute | solution.py:17
  597.2 26.1 %collective-permute-start.47 = (f32[6,68,2]{1,2,0:T(2,128)S(1)}, f32[6,68,2]{1,2,0:T(2,128)S(1)}, u32[]{:S(2)}, u32[]{:S(2)}) collective-permute-start(f32[6,68,2]{1,2,0:T(2,128)S(1)} %copy-done.286), channel_id=1, source_target_pairs={{1,0},{2,1},{3,2},{5,4},{6,5},{7,6},{9,8},{10,9},{11,10},{13,12},{... | collective-permute-start | bytes 9800 | tf_op jit(solution)/shard_map/ppermute | solution.py:20
  613.3 17.0 %collective-permute-start.32 = (f32[6,1,128]{1,2,0:T(8,128)}, f32[6,1,128]{1,2,0:T(8,128)}, u32[]{:S(2)}, u32[]{:S(2)}) collective-permute-start(f32[6,1,128]{1,2,0:T(8,128)} %get-tuple-element.195), channel_id=1, source_target_pairs={{0,4},{4,8},{8,12},{12,16},{16,20},{20,24},{24,28},{1,5},{5,9},{9,... | collective-permute-start | bytes 9224 | tf_op jit(solution)/shard_map/ppermute | solution.py:17
  621.2 84.6 %collective-permute-start.43 = (f32[6,68,2]{2,1,0:T(8,128)}, f32[6,68,2]{2,1,0:T(8,128)}, u32[]{:S(2)}, u32[]{:S(2)}) collective-permute-start(f32[6,68,2]{2,1,0:T(8,128)} %get-tuple-element.254), channel_id=1, source_target_pairs={{1,0},{2,1},{3,2},{5,4},{6,5},{7,6},{9,8},{10,9},{11,10},{13,12},{... | collective-permute-start | bytes 9800 | tf_op jit(solution)/shard_map/ppermute | solution.py:20
  623.3 97.1 %collective-permute-start.54 = (f32[6,68,2]{2,1,0:T(8,128)}, f32[6,68,2]{2,1,0:T(8,128)}, u32[]{:S(2)}, u32[]{:S(2)}) collective-permute-start(f32[6,68,2]{2,1,0:T(8,128)} %get-tuple-element.255), channel_id=1, source_target_pairs={{0,1},{1,2},{2,3},{4,5},{5,6},{6,7},{8,9},{9,10},{10,11},{12,13},{... | collective-permute-start | bytes 9800 | tf_op jit(solution)/shard_map/ppermute | solution.py:17
  698.3 22.1 %collective-permute-start.55 = (f32[6,68,2]{2,1,0:T(8,128)}, f32[6,68,2]{2,1,0:T(8,128)}, u32[]{:S(2)}, u32[]{:S(2)}) collective-permute-start(f32[6,68,2]{2,1,0:T(8,128)} %get-tuple-element.256), channel_id=1, source_target_pairs={{1,0},{2,1},{3,2},{5,4},{6,5},{7,6},{9,8},{10,9},{11,10},{13,12},{... | collective-permute-start | bytes 9800 | tf_op jit(solution)/shard_map/ppermute | solution.py:20
  714.7 112.8 %collective-permute-start.74 = (f32[6,36,2]{2,1,0:T(8,128)}, f32[6,36,2]{2,1,0:T(8,128)}, u32[]{:S(2)}, u32[]{:S(2)}) collective-permute-start(f32[6,36,2]{2,1,0:T(8,128)} %get-tuple-element.313), channel_id=1, source_target_pairs={{0,1},{1,2},{2,3},{4,5},{5,6},{6,7},{8,9},{9,10},{10,11},{12,13},{... | collective-permute-start | bytes 5192 | tf_op jit(solution)/shard_map/ppermute | solution.py:17
  742.2 30.3 %collective-permute-start.78 = (f32[6,36,2]{1,2,0:T(2,128)}, f32[6,36,2]{1,2,0:T(2,128)}, u32[]{:S(2)}, u32[]{:S(2)}) collective-permute-start(f32[6,36,2]{1,2,0:T(2,128)} %get-tuple-element.347), channel_id=1, source_target_pairs={{0,1},{1,2},{2,3},{4,5},{5,6},{6,7},{8,9},{9,10},{10,11},{12,13},{... | collective-permute-start | bytes 5192 | tf_op jit(solution)/shard_map/ppermute | solution.py:17
  746.7 28.5 %collective-permute-start.79 = (f32[6,36,2]{1,2,0:T(2,128)}, f32[6,36,2]{1,2,0:T(2,128)}, u32[]{:S(2)}, u32[]{:S(2)}) collective-permute-start(f32[6,36,2]{1,2,0:T(2,128)} %get-tuple-element.348), channel_id=1, source_target_pairs={{1,0},{2,1},{3,2},{5,4},{6,5},{7,6},{9,8},{10,9},{11,10},{13,12},{... | collective-permute-start | bytes 5192 | tf_op jit(solution)/shard_map/ppermute | solution.py:20
  765.5 16.9 %collective-permute-start.64 = (f32[6,1,64]{2,1,0:T(1,128)S(1)}, f32[6,1,64]{2,1,0:T(1,128)S(1)}, u32[]{:S(2)}, u32[]{:S(2)}) collective-permute-start(f32[6,1,64]{2,1,0:T(1,128)S(1)} %get-tuple-element.247), channel_id=1, source_target_pairs={{0,4},{4,8},{8,12},{12,16},{16,20},{20,24},{24,28},{1,5},{5,9},{9,... | collective-permute-start | bytes 4616 | tf_op jit(solution)/shard_map/ppermute | solution.py:17
  772.4 56.3 %collective-permute-start.75 = (f32[6,36,2]{2,1,0:T(8,128)}, f32[6,36,2]{2,1,0:T(8,128)}, u32[]{:S(2)}, u32[]{:S(2)}) collective-permute-start(f32[6,36,2]{2,1,0:T(8,128)} %get-tuple-element.314), channel_id=1, source_target_pairs={{1,0},{2,1},{3,2},{5,4},{6,5},{7,6},{9,8},{10,9},{11,10},{13,12},{... | collective-permute-start | bytes 5192 | tf_op jit(solution)/shard_map/ppermute | solution.py:20
  775.2 67.4 %collective-permute-start.86 = (f32[6,36,2]{2,1,0:T(8,128)}, f32[6,36,2]{2,1,0:T(8,128)}, u32[]{:S(2)}, u32[]{:S(2)}) collective-permute-start(f32[6,36,2]{2,1,0:T(8,128)} %get-tuple-element.315), channel_id=1, source_target_pairs={{0,1},{1,2},{2,3},{4,5},{5,6},{6,7},{8,9},{9,10},{10,11},{12,13},{... | collective-permute-start | bytes 5192 | tf_op jit(solution)/shard_map/ppermute | solution.py:17
  821.3 21.3 %collective-permute-start.87 = (f32[6,36,2]{2,1,0:T(8,128)}, f32[6,36,2]{2,1,0:T(8,128)}, u32[]{:S(2)}, u32[]{:S(2)}) collective-permute-start(f32[6,36,2]{2,1,0:T(8,128)} %get-tuple-element.316), channel_id=1, source_target_pairs={{1,0},{2,1},{3,2},{5,4},{6,5},{7,6},{9,8},{10,9},{11,10},{13,12},{... | collective-permute-start | bytes 5192 | tf_op jit(solution)/shard_map/ppermute | solution.py:20
  837.2 103.4 %collective-permute-start.106 = (f32[6,20,2]{2,1,0:T(8,128)}, f32[6,20,2]{2,1,0:T(8,128)}, u32[]{:S(2)}, u32[]{:S(2)}) collective-permute-start(f32[6,20,2]{2,1,0:T(8,128)} %get-tuple-element.379), channel_id=1, source_target_pairs={{0,1},{1,2},{2,3},{4,5},{5,6},{6,7},{8,9},{9,10},{10,11},{12,13},{... | collective-permute-start | bytes 2888 | tf_op jit(solution)/shard_map/ppermute | solution.py:17
  847.9 16.0 %collective-permute-start.88 = (f32[6,2,32]{2,1,0:T(2,128)}, f32[6,2,32]{2,1,0:T(2,128)S(1)}, u32[]{:S(2)}, u32[]{:S(2)}) collective-permute-start(f32[6,2,32]{2,1,0:T(2,128)} %get-tuple-element.311), channel_id=1, source_target_pairs={{0,4},{4,8},{8,12},{12,16},{16,20},{20,24},{24,28},{1,5},{5,9},{9,... | collective-permute-start | bytes 4616 | tf_op jit(solution)/shard_map/ppermute | solution.py:17
  863.9 26.3 %collective-permute-start.110 = (f32[6,20,2]{1,2,0:T(2,128)}, f32[6,20,2]{1,2,0:T(2,128)}, u32[]{:S(2)}, u32[]{:S(2)}) collective-permute-start(f32[6,20,2]{1,2,0:T(2,128)} %get-tuple-element.419), channel_id=1, source_target_pairs={{0,1},{1,2},{2,3},{4,5},{5,6},{6,7},{8,9},{9,10},{10,11},{12,13},{... | collective-permute-start | bytes 2888 | tf_op jit(solution)/shard_map/ppermute | solution.py:17
  868.5 24.4 %collective-permute-start.111 = (f32[6,20,2]{1,2,0:T(2,128)}, f32[6,20,2]{1,2,0:T(2,128)}, u32[]{:S(2)}, u32[]{:S(2)}) collective-permute-start(f32[6,20,2]{1,2,0:T(2,128)} %get-tuple-element.420), channel_id=1, source_target_pairs={{1,0},{2,1},{3,2},{5,4},{6,5},{7,6},{9,8},{10,9},{11,10},{13,12},{... | collective-permute-start | bytes 2888 | tf_op jit(solution)/shard_map/ppermute | solution.py:20
  882.5 17.9 %collective-permute-start.96 = (f32[6,1,32]{2,1,0:T(1,128)}, f32[6,1,32]{2,1,0:T(1,128)S(1)}, u32[]{:S(2)}, u32[]{:S(2)}) collective-permute-start(f32[6,1,32]{2,1,0:T(1,128)} %get-tuple-element.307), channel_id=1, source_target_pairs={{0,4},{4,8},{8,12},{12,16},{16,20},{20,24},{24,28},{1,5},{5,9},{9,... | collective-permute-start | bytes 2312 | tf_op jit(solution)/shard_map/ppermute | solution.py:17
  890.2 51.7 %collective-permute-start.107 = (f32[6,20,2]{2,1,0:T(8,128)}, f32[6,20,2]{2,1,0:T(8,128)}, u32[]{:S(2)}, u32[]{:S(2)}) collective-permute-start(f32[6,20,2]{2,1,0:T(8,128)} %get-tuple-element.380), channel_id=1, source_target_pairs={{1,0},{2,1},{3,2},{5,4},{6,5},{7,6},{9,8},{10,9},{11,10},{13,12},{... | collective-permute-start | bytes 2888 | tf_op jit(solution)/shard_map/ppermute | solution.py:20
  892.9 64.1 %collective-permute-start.118 = (f32[6,20,2]{2,1,0:T(8,128)}, f32[6,20,2]{2,1,0:T(8,128)}, u32[]{:S(2)}, u32[]{:S(2)}) collective-permute-start(f32[6,20,2]{2,1,0:T(8,128)} %get-tuple-element.381), channel_id=1, source_target_pairs={{0,1},{1,2},{2,3},{4,5},{5,6},{6,7},{8,9},{9,10},{10,11},{12,13},{... | collective-permute-start | bytes 2888 | tf_op jit(solution)/shard_map/ppermute | solution.py:17
  934.0 26.6 %collective-permute-start.119 = (f32[6,20,2]{2,1,0:T(8,128)}, f32[6,20,2]{2,1,0:T(8,128)}, u32[]{:S(2)}, u32[]{:S(2)}) collective-permute-start(f32[6,20,2]{2,1,0:T(8,128)} %get-tuple-element.382), channel_id=1, source_target_pairs={{1,0},{2,1},{3,2},{5,4},{6,5},{7,6},{9,8},{10,9},{11,10},{13,12},{... | collective-permute-start | bytes 2888 | tf_op jit(solution)/shard_map/ppermute | solution.py:20
  941.9 20.0 %collective-permute-start.102 = (f32[6,20,2]{2,1,0:T(8,128)}, f32[6,20,2]{2,1,0:T(8,128)}, u32[]{:S(2)}, u32[]{:S(2)}) collective-permute-start(f32[6,20,2]{2,1,0:T(8,128)} %get-tuple-element.383), channel_id=1, source_target_pairs={{0,1},{1,2},{2,3},{4,5},{5,6},{6,7},{8,9},{9,10},{10,11},{12,13},{... | collective-permute-start | bytes 2888 | tf_op jit(solution)/shard_map/ppermute | solution.py:17
  946.6 19.4 %collective-permute-start.103 = (f32[6,20,2]{2,1,0:T(8,128)}, f32[6,20,2]{2,1,0:T(8,128)}, u32[]{:S(2)}, u32[]{:S(2)}) collective-permute-start(f32[6,20,2]{2,1,0:T(8,128)} %get-tuple-element.384), channel_id=1, source_target_pairs={{1,0},{2,1},{3,2},{5,4},{6,5},{7,6},{9,8},{10,9},{11,10},{13,12},{... | collective-permute-start | bytes 2888 | tf_op jit(solution)/shard_map/ppermute | solution.py:20
  951.0 139.2 %collective-permute-start.170 = (f32[6,8,2]{0,2,1:T(2,128)}, f32[6,8,2]{0,2,1:T(2,128)}, u32[]{:S(2)}, u32[]{:S(2)}) collective-permute-start(f32[6,8,2]{0,2,1:T(2,128)} %get-tuple-element.481), channel_id=1, source_target_pairs={{0,1},{1,2},{2,3},{4,5},{5,6},{6,7},{8,9},{9,10},{10,11},{12,13},{... | collective-permute-start | bytes 1160 | tf_op jit(solution)/shard_map/ppermute | solution.py:17
  957.0 37.9 %collective-permute-start.138 = (f32[6,12,2]{0,2,1:T(2,128)}, f32[6,12,2]{0,2,1:T(2,128)S(1)}, u32[]{:S(2)}, u32[]{:S(2)}) collective-permute-start(f32[6,12,2]{0,2,1:T(2,128)} %get-tuple-element.401), channel_id=1, source_target_pairs={{0,1},{1,2},{2,3},{4,5},{5,6},{6,7},{8,9},{9,10},{10,11},{12,13},{... | collective-permute-start | bytes 1736 | tf_op jit(solution)/shard_map/ppermute | solution.py:17
  960.6 37.6 %collective-permute-start.139 = (f32[6,12,2]{0,2,1:T(2,128)}, f32[6,12,2]{0,2,1:T(2,128)S(1)}, u32[]{:S(2)}, u32[]{:S(2)}) collective-permute-start(f32[6,12,2]{0,2,1:T(2,128)} %get-tuple-element.402), channel_id=1, source_target_pairs={{1,0},{2,1},{3,2},{5,4},{6,5},{7,6},{9,8},{10,9},{11,10},{13,12},{... | collective-permute-start | bytes 1736 | tf_op jit(solution)/shard_map/ppermute | solution.py:20
  987.2 33.7 %collective-permute-start.150 = (f32[6,12,2]{0,2,1:T(2,128)}, f32[6,12,2]{0,2,1:T(2,128)S(1)}, u32[]{:S(2)}, u32[]{:S(2)}) collective-permute-start(f32[6,12,2]{0,2,1:T(2,128)} %get-tuple-element.405), channel_id=1, source_target_pairs={{0,1},{1,2},{2,3},{4,5},{5,6},{6,7},{8,9},{9,10},{10,11},{12,13},{... | collective-permute-start | bytes 1736 | tf_op jit(solution)/shard_map/ppermute | solution.py:17
  991.3 30.9 %collective-permute-start.151 = (f32[6,12,2]{0,2,1:T(2,128)}, f32[6,12,2]{0,2,1:T(2,128)S(1)}, u32[]{:S(2)}, u32[]{:S(2)}) collective-permute-start(f32[6,12,2]{0,2,1:T(2,128)} %get-tuple-element.406), channel_id=1, source_target_pairs={{1,0},{2,1},{3,2},{5,4},{6,5},{7,6},{9,8},{10,9},{11,10},{13,12},{... | collective-permute-start | bytes 1736 | tf_op jit(solution)/shard_map/ppermute | solution.py:20
  1009.9 17.2 %collective-permute-start.126 = (f32[6,12,2]{0,2,1:T(2,128)}, f32[6,12,2]{0,2,1:T(2,128)}, u32[]{:S(2)}, u32[]{:S(2)}) collective-permute-start(f32[6,12,2]{0,2,1:T(2,128)} %get-tuple-element.399), channel_id=1, source_target_pairs={{0,1},{1,2},{2,3},{4,5},{5,6},{6,7},{8,9},{9,10},{10,11},{12,13},{... | collective-permute-start | bytes 1736 | tf_op jit(solution)/shard_map/ppermute | solution.py:17
  1020.9 72.6 %collective-permute-start.171 = (f32[6,8,2]{0,2,1:T(2,128)}, f32[6,8,2]{0,2,1:T(2,128)S(1)}, u32[]{:S(2)}, u32[]{:S(2)}) collective-permute-start(f32[6,8,2]{0,2,1:T(2,128)} %get-tuple-element.482), channel_id=1, source_target_pairs={{1,0},{2,1},{3,2},{5,4},{6,5},{7,6},{9,8},{10,9},{11,10},{13,12},{... | collective-permute-start | bytes 1160 | tf_op jit(solution)/shard_map/ppermute | solution.py:20
  1022.2 81.0 %collective-permute-start.182 = (f32[6,8,2]{0,2,1:T(2,128)}, f32[6,8,2]{0,2,1:T(2,128)S(1)}, u32[]{:S(2)}, u32[]{:S(2)}) collective-permute-start(f32[6,8,2]{0,2,1:T(2,128)} %get-tuple-element.483), channel_id=1, source_target_pairs={{0,1},{1,2},{2,3},{4,5},{5,6},{6,7},{8,9},{9,10},{10,11},{12,13},{... | collective-permute-start | bytes 1160 | tf_op jit(solution)/shard_map/ppermute | solution.py:17
  1083.9 26.7 %collective-permute-start.183 = (f32[6,8,2]{0,2,1:T(2,128)S(1)}, f32[6,8,2]{0,2,1:T(2,128)S(1)}, u32[]{:S(2)}, u32[]{:S(2)}) collective-permute-start(f32[6,8,2]{0,2,1:T(2,128)S(1)} %copy-done.280), channel_id=1, source_target_pairs={{1,0},{2,1},{3,2},{5,4},{6,5},{7,6},{9,8},{10,9},{11,10},{13,12},{... | collective-permute-start | bytes 1160 | tf_op jit(solution)/shard_map/ppermute | solution.py:20
  1086.9 17.6 %collective-permute-start.174 = (f32[6,8,2]{0,2,1:T(2,128)S(1)}, f32[6,8,2]{0,2,1:T(2,128)S(1)}, u32[]{:S(2)}, u32[]{:S(2)}) collective-permute-start(f32[6,8,2]{0,2,1:T(2,128)S(1)} %copy-done.284), channel_id=1, source_target_pairs={{0,1},{1,2},{2,3},{4,5},{5,6},{6,7},{8,9},{9,10},{10,11},{12,13},{... | collective-permute-start | bytes 1160 | tf_op jit(solution)/shard_map/ppermute | solution.py:17
  (496 other events, 13686.5 us)
where the time goes:
time: 1550 us; the launch traced here: 1530 us
  starting transfers between devices  662 us (43%)
  local copies, waits for them, and re-layouts  344 us (22%)
  other arithmetic  254 us (16%)
  waiting for transfers between devices  153 us (10%)
  blocking collectives  79.5 us (5%)
  between operations  36.8 us (2%)
    ppermute x120, starting transfers between devices, extended(): lax.ppermute(lax.slice_in_dim(block, block.shape[dim] - width, None, axis...  463 us
    ppermute x120, starting transfers between devices, extended(): lax.ppermute(lax.slice_in_dim(block, 0, width, axis=dim), axis, backward)  199 us
    ppermute x120, waiting for transfers between devices, extended(): lax.ppermute(lax.slice_in_dim(block, 0, width, axis=dim), axis, backward)  139 us
    unnamed x658, local copies, waits for them, and re-layouts  122 us
    slice x19, local copies, waits for them, and re-layouts, restrict(): blocks[:, :, 1, :, 0]  77 us
    select_n x48, other arithmetic, update(): return jnp.where(chosen, candidate, beside_all)  54.1 us
    add x3, other arithmetic, lookup(): summed = summed + jnp.where(labels == number, entries[number], 0.0)  50.2 us
    concatenate x83, other arithmetic, extended(): block = jnp.concatenate([low, block, high], axis=dim)  36 us
  transfers between devices with their start and end apart: 240, of which 60 were waited for; matrix products, arithmetic and copies ran while one was open for 31% of the time, Pallas kernels for 0%

commit v1 on v0

v1 whole, which is shorter than its diff:
```python
import functools

import jax
import jax.numpy as jnp
from jax import lax
from jax.experimental import pallas as pl
from jax.experimental.pallas import tpu as pltpu
from jax.sharding import PartitionSpec as P

TILE = 16
LEVELS = 6
SWEEPS = 2
COARSE_ITERS = 12
LOCAL = 3
FRAME = 64
WIDE = 56
PAD = 8
F32 = jnp.float32
VM = 60 * 1024 * 1024


def up_to(count, step):
    return -(-count // step) * step


def spans(low, high, columns):
    step = max(8, 8 * (4096 // columns // 8) * 2)
    return [(r, min(step, high - r)) for r in range(low, high, step)]


def split_dot(matrix_left, values, matrix_right):
    def parts(x):
        a = x.astype(jnp.bfloat16)
        x = x - a.astype(F32)
        b = x.astype(jnp.bfloat16)
        x = x - b.astype(F32)
        return a, b, x.astype(jnp.bfloat16)

    dot = functools.partial(jnp.dot, preferred_element_type=F32)
    a, b, c = parts(values)
    values = (dot(matrix_left, c) + dot(matrix_left, b)) + dot(matrix_left, a)
    a, b, c = parts(values)
    return (dot(c, matrix_right) + dot(b, matrix_right)) + dot(a, matrix_right)


def pairs(rows, columns, weight, tall):
    r = lax.broadcasted_iota(jnp.int32, (rows, columns), 0)
    c = lax.broadcasted_iota(jnp.int32, (rows, columns), 1)
    hit = (r // 2 == c) if tall else (c // 2 == r)
    return jnp.where(hit, F32(weight), F32(0.0)).astype(jnp.bfloat16)


def restrict(fine, coarse, layers_fine, layers_coarse):
    rf, cf = fine.shape[1] - 2 * PAD, fine.shape[2]
    rc, cc = coarse.shape[1] - 2 * PAD, coarse.shape[2]
    left = pairs(rc, rf, 0.5, False)
    right = pairs(cf, cc, 0.5, True)

    def body(k, carry):
        x = fine[k + layers_fine, PAD : PAD + rf, :]
        coarse[k + layers_coarse, PAD : PAD + rc, :] = split_dot(left, x, right)
        return carry

    lax.fori_loop(0, 6, body, 0)


def prolong_add(coarse, fine):
    rf, cf = fine.shape[1] - 2 * PAD, fine.shape[2]
    rc, cc = coarse.shape[1] - 2 * PAD, coarse.shape[2]
    left = pairs(rf, rc, 1.0, True)
    right = pairs(cc, cf, 1.0, False)

    def body(k, carry):
        x = coarse[k + 1, PAD : PAD + rc, :]
        fine[k + 1, PAD : PAD + rf, :] += split_dot(left, x, right)
        return carry

    lax.fori_loop(0, 6, body, 0)


def build(coef, weights, scale):
    lat, ver, sto = coef
    wr, wc, wv, inv, diag = weights
    rows, columns = lat.shape[1] - 2 * PAD, lat.shape[2]
    half = F32(0.5 * scale)
    wr[...] = jnp.zeros_like(wr)
    wv[0] = jnp.zeros(wv.shape[1:], F32)
    wv[6] = jnp.zeros(wv.shape[1:], F32)

    def faces(k, carry):
        for r, n in spans(PAD, PAD + rows, columns):
            here = lat[k, r : r + n, :]
            wr[k, r : r + n, :] = half * (here + lat[k, r - 1 : r - 1 + n, :])
            wc[k, r : r + n, :] = half * (here + pltpu.roll(here, 1, 1))
        wr[k, PAD + rows : PAD + rows + 8, :] = half * (
            lat[k, PAD + rows : PAD + rows + 8, :]
            + lat[k, PAD + rows - 1 : PAD + rows + 7, :]
        )
        return carry

    lax.fori_loop(0, 6, faces, 0)

    def layer(k, carry):
        for r, n in spans(PAD, PAD + rows, columns):
            wv[k, r : r + n, :] = F32(0.5) * (ver[k, r : r + n, :] + ver[k - 1, r : r + n, :])
        return carry

    lax.fori_loop(1, 6, layer, 0)

    def total(k, carry):
        for r, n in spans(PAD, PAD + rows, columns):
            left = wc[k, r : r + n, :]
            s = sto[k, r : r + n, :]
            d = s + wr[k, r : r + n, :] + wr[k, r + 1 : r + 1 + n, :]
            d = d + left + pltpu.roll(left, columns - 1, 1)
            d = d + wv[k, r : r + n, :] + wv[k + 1, r : r + n, :]
            diag[k, r : r + n, :] = d
            inv[k, r : r + n, :] = jnp.where(s > 0.0, F32(1.0) / jnp.where(s > 0.0, d, 1.0), 0.0)
        return carry

    lax.fori_loop(0, 6, total, 0)


def beside(u, weights, k, r, n, here):
    wr, wc, wv = weights[:3]
    columns = u.shape[2]
    left = wc[k, r : r + n, :]
    summed = wr[k, r : r + n, :] * u[k + 1, r - 1 : r - 1 + n, :]
    summed += wr[k, r + 1 : r + 1 + n, :] * u[k + 1, r + 1 : r + 1 + n, :]
    summed += left * pltpu.roll(here, 1, 1)
    summed += pltpu.roll(left * here, columns - 1, 1)
    summed += wv[k, r : r + n, :] * u[k, r : r + n, :]
    summed += wv[k + 1, r : r + n, :] * u[k + 2, r : r + n, :]
    return summed


def smooth(u, rhs, weights, low, high):
    inv = weights[3]
    columns = u.shape[2]

    def half_sweep(step, carry):
        colour = step % 2

        def layer(k, inner):
            for r, n in spans(PAD + low, PAD + high, columns):
                here = u[k + 1, r : r + n, :]
                new = (rhs[k, r : r + n, :] + beside(u, weights, k, r, n, here)) * inv[
                    k, r : r + n, :
                ]
                odd = lax.broadcasted_iota(jnp.int32, (n, columns), 0)
                odd = (odd + lax.broadcasted_iota(jnp.int32, (n, columns), 1) + k + colour) & 1
                u[k + 1, r : r + n, :] = jnp.where(odd == 0, new, here)
            return inner

        return lax.fori_loop(0, 6, layer, carry)

    lax.fori_loop(0, 2 * SWEEPS, half_sweep, 0)


def residual(u, rhs, weights, out):
    diag = weights[4]
    rows, columns = u.shape[1] - 2 * PAD, u.shape[2]

    def layer(k, carry):
        for r, n in spans(PAD, PAD + rows, columns):
            here = u[k + 1, r : r + n, :]
            out[k, r : r + n, :] = rhs[k, r : r + n, :] - (
                diag[k, r : r + n, :] * here - beside(u, weights, k, r, n, here)
            )
        return carry

    lax.fori_loop(0, 6, layer, 0)


def down_level(index, u, rhs, coef, weights, temp, nxt_rhs, nxt_coef, low, high):
    if index > 0:
        u[...] = jnp.zeros_like(u)
    build(coef, weights, 0.25**index)
    smooth(u, rhs, weights, low, high)
    residual(u, rhs, weights, temp)
    restrict(temp, nxt_rhs, 0, 0)
    for mine, following in zip(coef, nxt_coef):
        following[...] = jnp.zeros_like(following)
        restrict(mine, following, 0, 0)


def down_kernel(x_ref, lat_t, ver_t, sto_t, *refs):
    outs, scratch = refs[: 6 * LOCAL + 4], refs[6 * LOCAL + 4 :]
    level = [outs[6 * i : 6 * i + 6] for i in range(LOCAL)]
    coarse = outs[6 * LOCAL :]
    own = [scratch[5 * i : 5 * i + 5] for i in range(LOCAL)]
    u, rhs = level[0][:2]
    lat, ver, sto = own[0][:3]
    rows, columns = x_ref.shape[1:]
    for ref in (u, lat):
        ref[...] = jnp.zeros_like(ref)

    def look(k, carry):
        for r, n in spans(0, rows, columns):
            labels = x_ref[k + 6, r : r + n, :]
            a = jnp.zeros((n, columns), F32)
            b, c = a, a
            for m in range(lat_t.shape[0]):
                hit = labels == F32(m + 1)
                a = jnp.where(hit, lat_t[m], a)
                b = jnp.where(hit, ver_t[m], b)
                c = jnp.where(hit, sto_t[m], c)
            t = x_ref[k, r : r + n, :]
            lat[k, r + PAD : r + PAD + n, :] = a
            ver[k, r + PAD : r + PAD + n, :] = b
            sto[k, r + PAD : r + PAD + n, :] = c
            u[k + 1, r + PAD : r + PAD + n, :] = t
            rhs[k, r + PAD : r + PAD + n, :] = c * t
        return carry

    lax.fori_loop(0, 6, look, 0)
    rhs[0, PAD : PAD + rows, :] += x_ref[12]
    for i in range(LOCAL):
        last = i == LOCAL - 1
        size = level[i][0].shape[1] - 2 * PAD
        cut = 8 if i < 2 else 0
        down_level(
            i,
            level[i][0],
            level[i][1],
            own[i][:3],
            level[i][2:6] + own[i][3:4],
            own[i][4],
            coarse[0] if last else level[i + 1][1],
            coarse[1:4] if last else own[i + 1][:3],
            cut,
            size - cut,
        )


def coarse_kernel(g_ref, out_ref, *scratch):
    count = LEVELS - LOCAL
    rows, columns = g_ref.shape[1:]
    data = [scratch[11 * i : 11 * i + 11] for i in range(count + 1)]
    for j in range(4):
        ref = data[0][(1, 6, 7, 8)[j]]
        ref[...] = jnp.zeros_like(ref)

        def take(k, carry, ref=ref, j=j):
            ref[k, PAD : PAD + rows, :] = g_ref[6 * j + k]
            return carry

        lax.fori_loop(0, 6, take, 0)
    for i in range(count):
        u, rhs, wr, wc, wv, inv, lat, ver, sto, diag, temp = data[i]
        down_level(
            LOCAL + i, u, rhs, (lat, ver, sto), (wr, wc, wv, inv, diag), temp,
            data[i + 1][1], data[i + 1][6:9], 0, u.shape[1] - 2 * PAD,
        )
    u, rhs, wr, wc, wv, inv, lat, ver, sto, diag, temp = data[count]
    build((lat, ver, sto), (wr, wc, wv, inv, diag), 0.25**LEVELS)
    n, columns = u.shape[1] - 2 * PAD, u.shape[2]
    u[...] = jnp.zeros_like(u)
    mid = slice(PAD, PAD + n)

    def summed(x):
        x = jnp.sum(x, axis=0)
        return jnp.sum(jnp.sum(x, axis=0, keepdims=True), axis=1, keepdims=True)

    r0 = rhs[:, mid, :]
    z0 = r0 * inv[:, mid, :]
    u[1:7, mid, :] = z0
    temp[:, mid, :] = r0
    lat[:, mid, :] = jnp.zeros_like(r0)

    def step(_, rz):
        p = u[1:7, mid, :]
        image = jnp.stack(
            [diag[k, mid, :] * p[k] - beside(u, (wr, wc, wv), k, PAD, n, p[k]) for k in range(6)]
        )
        alpha = rz / summed(p * image)
        lat[:, mid, :] += alpha[None] * p
        r = temp[:, mid, :] - alpha[None] * image
        temp[:, mid, :] = r
        z = r * inv[:, mid, :]
        rz_new = summed(r * z)
        u[1:7, mid, :] = z + (rz_new / rz)[None] * p
        return rz_new

    lax.fori_loop(0, COARSE_ITERS, step, summed(r0 * z0))
    u[1:7, mid, :] = lat[:, mid, :]
    for i in reversed(range(count)):
        u, rhs, wr, wc, wv, inv = data[i][:6]
        prolong_add(data[i + 1][0], u)
        smooth(u, rhs, (wr, wc, wv, inv), 0, u.shape[1] - 2 * PAD)
    u = data[0][0]

    def give(k, carry):
        out_ref[k] = u[k + 1, PAD : PAD + rows, :]
        return carry

    lax.fori_loop(0, 6, give, 0)


def up_kernel(e_ref, *refs):
    ins = refs[: 6 * LOCAL]
    out_ref = refs[6 * LOCAL]
    us = refs[6 * LOCAL + 1 :]
    correction = e_ref
    for i in reversed(range(LOCAL)):
        u, rhs, wr, wc, wv, inv = ins[6 * i : 6 * i + 6]
        mine = us[i]
        mine[...] = u[...]
        prolong_add(correction, mine)
        size = u.shape[1] - 2 * PAD
        cut = (56, 24, 8)[i]
        smooth(mine, rhs, (wr, wc, wv, inv), cut, size - cut)
        correction = mine
    rows, columns = out_ref.shape[1:]
    wide = correction.shape[2]

    def give(k, carry):
        x = correction[k + 1, PAD + FRAME : PAD + FRAME + rows, :]
        out_ref[k] = pltpu.roll(x, wide - FRAME, 1)[:, :columns]
        return carry

    lax.fori_loop(0, 6, give, 0)


def extended(block, axis, dim):
    count = lax.axis_size(axis)
    forward = [(i, i + 1) for i in range(count - 1)]
    backward = [(target, source) for source, target in forward]
    size = block.shape[dim]
    low = lax.ppermute(lax.slice_in_dim(block, size - WIDE, None, axis=dim), axis, forward)
    high = lax.ppermute(lax.slice_in_dim(block, 0, WIDE, axis=dim), axis, backward)
    shape = list(block.shape)
    shape[dim] = FRAME - WIDE
    edge = jnp.zeros(shape, block.dtype)
    return jnp.concatenate([edge, low, block, high, edge], axis=dim)


def lookup(labels, entries):
    summed = jnp.zeros(labels.shape, entries.dtype)
    for number in range(entries.shape[0]):
        summed = summed + jnp.where(labels == number, entries[number], 0.0)
    return summed


def frame(layers, rows, columns):
    return (layers, rows + 2 * PAD, columns)


def on_device(field, substance, patch, planar, vertical, storage, wattage):
    heat = jnp.repeat(jnp.repeat(lookup(patch, wattage), TILE, axis=0), TILE, axis=1)
    x = jnp.concatenate([field, substance.astype(F32) + 1.0, heat[None]], 0)
    x = extended(extended(x, "gy", 2), "gx", 1)
    local_rows, local_cols = field.shape[1:]
    vmem = pl.BlockSpec(memory_space=pltpu.VMEM)
    smem = pl.BlockSpec(memory_space=pltpu.SMEM)
    params = pltpu.CompilerParams(vmem_limit_bytes=VM)
    dims = []
    for i in range(LOCAL + 1):
        dims.append(
            (
                up_to((local_rows + 2 * FRAME) >> i, 8),
                up_to((local_cols + 2 * FRAME) >> i, 128),
            )
        )
    shapes, scratch = [], []
    for i in range(LOCAL):
        shapes += [jax.ShapeDtypeStruct(frame(n, *dims[i]), F32) for n in (8, 6, 6, 6, 7, 6)]
        scratch += [pltpu.VMEM(frame(6, *dims[i]), F32) for _ in range(5)]
    coarse = [jax.ShapeDtypeStruct(frame(6, *dims[LOCAL]), F32)] * 4
    result = pl.pallas_call(
        down_kernel,
        out_shape=shapes + coarse,
        in_specs=[vmem] + [smem] * 3,
        out_specs=[vmem] * (6 * LOCAL + 4),
        scratch_shapes=scratch,
        compiler_params=params,
    )(x, planar, vertical, storage)
    levels, coarse = result[: 6 * LOCAL], result[6 * LOCAL :]
    h, w = local_rows >> LOCAL, local_cols >> LOCAL
    off = FRAME >> LOCAL
    mine = jnp.concatenate(
        [c[:, PAD + off : PAD + off + h, off : off + w] for c in coarse], 0
    )
    nx, ny = lax.axis_size("gx"), lax.axis_size("gy")
    all_blocks = lax.all_gather(mine, ("gx", "gy"), axis=0, tiled=False)
    all_blocks = all_blocks.reshape(nx, ny, 24, h, w).transpose(2, 0, 3, 1, 4)
    whole = all_blocks.reshape(24, nx * h, ny * w)
    sizes = [
        (up_to(((nx * h) >> i) + 1, 8), up_to(((ny * w) >> i) + 1, 128))
        for i in range(LEVELS - LOCAL + 1)
    ]
    whole = jnp.pad(
        whole, ((0, 0), (0, sizes[0][0] - nx * h), (0, sizes[0][1] - ny * w))
    )
    scratch = []
    for size in sizes:
        scratch += [
            pltpu.VMEM(frame(n, *size), F32) for n in (8, 6, 6, 6, 7, 6, 6, 6, 6, 6, 6)
        ]
    solved = pl.pallas_call(
        coarse_kernel,
        out_shape=jax.ShapeDtypeStruct((6,) + sizes[0], F32),
        in_specs=[vmem],
        out_specs=vmem,
        scratch_shapes=scratch,
        compiler_params=params,
    )(whole)
    solved = jnp.pad(solved, ((1, 1), (off, off), (off, off)))
    zero = jnp.int32(0)
    window = lax.dynamic_slice(
        solved,
        (zero, lax.axis_index("gx") * h, lax.axis_index("gy") * w),
        (8, h + 2 * off, w + 2 * off),
    )
    r3, c3 = dims[LOCAL]
    window = jnp.pad(window, ((0, 0), (PAD, PAD), (0, c3 - (w + 2 * off))))
    return pl.pallas_call(
        up_kernel,
        out_shape=jax.ShapeDtypeStruct(field.shape, F32),
        in_specs=[vmem] * (1 + 6 * LOCAL),
        out_specs=vmem,
        scratch_shapes=[pltpu.VMEM(frame(8, *dims[i]), F32) for i in range(LOCAL)],
        compiler_params=params,
    )(window, *levels)


def solution(mesh):
    placed = (P(None, "gx", "gy"), P(None, "gx", "gy"), P("gx", "gy"), P(), P(), P(), P())
    return jax.shard_map(
        on_device, mesh=mesh, in_specs=placed, out_specs=P(None, "gx", "gy"), check_vma=False
    )
```

time: 1550 us -> 402 us (0.26); the launches traced: 1530 us -> 400 us
  starting transfers between devices: 662 us -> 11.8 us
  local copies, waits for them, and re-layouts: 344 us -> 39.3 us
  other arithmetic: 254 us -> 42.8 us
  Pallas kernels: 0 us -> 133 us
  waiting for transfers between devices: 153 us -> 21.2 us
  blocking collectives: 79.5 us -> 151 us
  between operations: 36.8 us -> 0.14 us
    ppermute x240 -> x4, starting transfers between devices: 662 us -> 11.8 us  [the longest x2 8.56 us: extended(): lax.ppermute(lax.slice_in_dim(block, size - WIDE, None, axis=dim), axis,...]
    pallas_call x0 -> x3, Pallas kernels: none -> 133 us  [the longest x1 57.5 us: on_device(): pl.pallas_call(coarse_kernel, out_shape=jax.ShapeDtypeStruct((6,) + sizes...]
    ppermute x240 -> x4, waiting for transfers between devices: 153 us -> 21.2 us  [the longest x2 11.9 us: extended(): lax.ppermute(lax.slice_in_dim(block, size - WIDE, None, axis=dim), axis,...]
    slice x154 -> x8, local copies, waits for them, and re-layouts: 129 us -> 5.4 us  [the longest x4 3.52 us: on_device(): c[:, PAD + off:PAD + off + h, off:off + w]]
    unnamed x658 -> x4, local copies, waits for them, and re-layouts: 122 us -> 5.14 us
    all_gather x8 -> x1, blocking collectives: 79.5 us -> 151 us  [on_device(): all_blocks = lax.all_gather(mine, ('gx', 'gy'), axis=0, tiled=False)]
    select_n x49 -> x0, other arithmetic: 55.6 us -> none  [the longest x48 54.1 us: update(): return jnp.where(chosen, candidate, beside_all)]
    reduce_sum x23 -> x0, other arithmetic: 46.2 us -> none  [the longest x12 24.9 us: conjugate(): alpha_step = inner / jnp.sum(search * image)]
  transfers between devices with their start and end apart: 240 -> 4, of which waited for: 60 -> 4; matrix products, arithmetic and copies ran while one was open for 31% -> 1% of each run, Pallas kernels for 0% -> 0%
where the time goes in v1:
time: 402 us; the launch traced here: 400 us
  blocking collectives  151 us (38%)
  Pallas kernels  133 us (33%)
  other arithmetic  42.8 us (11%)
  local copies, waits for them, and re-layouts  39.3 us (10%)
  waiting for transfers between devices  21.2 us (5%)
  starting transfers between devices  11.8 us (3%)
    all_gather x1, blocking collectives, on_device(): all_blocks = lax.all_gather(mine, ('gx', 'gy'), axis=0, tiled=False)  151 us
    pallas_call x1, Pallas kernels, on_device(): pl.pallas_call(coarse_kernel, out_shape=jax.ShapeDtypeStruct((6,) + sizes...  57.5 us
    pallas_call x1, Pallas kernels, on_device(): pl.pallas_call(down_kernel, out_shape=shapes + coarse, in_specs=[vmem] +...  53.3 us
    add x1, other arithmetic, lookup(): summed = summed + jnp.where(labels == number, entries[number], 0.0)  40.6 us
    pallas_call x1, Pallas kernels, on_device(): pl.pallas_call(up_kernel, out_shape=jax.ShapeDtypeStruct(field.shape, F32...  22.5 us
    ppermute x2, waiting for transfers between devices, extended(): lax.ppermute(lax.slice_in_dim(block, size - WIDE, None, axis=dim), axis,...  11.9 us
    ppermute x2, waiting for transfers between devices, extended(): lax.ppermute(lax.slice_in_dim(block, 0, WIDE, axis=dim), axis, backward)  9.26 us
    ppermute x2, starting transfers between devices, extended(): lax.ppermute(lax.slice_in_dim(block, size - WIDE, None, axis=dim), axis,...  8.56 us
  transfers between devices with their start and end apart: 4, of which 4 were waited for; matrix products, arithmetic and copies ran while one was open for 1% of the time, Pallas kernels for 0%

profile of v1, /device:TPU:1, one launch (start us, length us, event | category | flops | bytes accessed | tf_op | source)
XLA Modules:
  0.0 399.7 jit_solution(13175846508312633984)
XLA Ops:
  0.0 2.1 fusion.2
  2.1 2.1 fusion.3
  4.1 2.1 fusion.4
  6.2 1.6 fusion.5
  7.8 40.6 %select_add_fusion = f32[8,8]{1,0:T(8,128)S(1)} fusion(s32[8,8]{1,0:T(8,128)} %param.9, f32[]{:T(128)} %bitcast.63, f32[]{:T(128)} %bitcast.62, f32[]{:T(128)} %bitcast.61, f32[]{:T(128)} %bitcast.60, f32[]{:T(128)} %bitcast.59, f32[]{:T(128)} %bitcast.58, f32[]{:T(128)} %bitcast.57, f32[]{:T(128)} %bitcast.56, f32[]{:T(128)} %bitcast.55, f32[]{:T(128)} %bitcast.54, ...), kind=kLoop, calls=%fused_computation.9 | loop fusion | flops 12224 | bytes 768 | tf_op jit(solution)/shard_map/add | solution.py:341
  48.4 0.1 copy.13
  48.5 0.1 broadcast_in_dim.339
  48.6 0.1 reshape.9
  48.7 0.1 copy.14
  48.8 1.0 convert_add_fusion
  49.8 1.1 pad_maximum_fusion
  50.9 0.3 fusion.1
  51.2 0.3 copy.15
  51.5 4.0 collective-permute-start
  55.4 0.3 copy.16
  55.7 1.3 collective-permute-start.1
  57.0 5.7 %collective-permute-done = f32[13,128,56]{1,2,0:T(8,128)S(1)} collective-permute-done((f32[13,128,56]{1,2,0:T(8,128)S(1)}, f32[13,128,56]{1,2,0:T(8,128)S(1)}, u32[]{:S(2)}, u32[]{:S(2)}) %collective-permute-start) | collective-permute-done | bytes 372768 | tf_op jit(solution)/shard_map/ppermute | solution.py:330
  62.7 1.2 copy.17
  64.0 8.7 %collective-permute-done.1 = f32[13,128,56]{1,2,0:T(8,128)S(1)} collective-permute-done((f32[13,128,56]{1,2,0:T(8,128)S(1)}, f32[13,128,56]{1,2,0:T(8,128)S(1)}, u32[]{:S(2)}, u32[]{:S(2)}) %collective-permute-start.1) | collective-permute-done | bytes 372768 | tf_op jit(solution)/shard_map/ppermute | solution.py:331
  72.7 1.2 copy.18
  73.9 0.1 broadcast_in_dim.273
  74.0 3.1 concatenate.13
  77.1 1.0 fusion
  78.1 4.6 %collective-permute-start.2 = (f32[13,56,256]{2,1,0:T(8,128)}, f32[13,56,256]{2,1,0:T(8,128)}, u32[]{:S(2)}, u32[]{:S(2)}) collective-permute-start(f32[13,56,256]{2,1,0:T(8,128)} %get-tuple-element.50), channel_id=1, source_target_pairs={{0,4},{4,8},{8,12},{12,16},{16,20},{20,24},{24,28},{1,5},{5,9},{9,... | collective-permute-start | bytes 2236424 | tf_op jit(solution)/shard_map/ppermute | solution.py:330
  82.8 1.9 collective-permute-start.3
  84.7 0.7 broadcast_dynamic-update-slice_fusion
  85.4 6.2 %collective-permute-done.2 = f32[13,56,256]{2,1,0:T(8,128)} collective-permute-done((f32[13,56,256]{2,1,0:T(8,128)}, f32[13,56,256]{2,1,0:T(8,128)}, u32[]{:S(2)}, u32[]{:S(2)}) %collective-permute-start.2) | collective-permute-done | bytes 745504 | tf_op jit(solution)/shard_map/ppermute | solution.py:330
  91.5 2.1 constant_dynamic-update-slice_fusion.2
  93.6 1.4 constant_dynamic-update-slice_fusion.1
  95.1 0.6 collective-permute-done.3
  95.6 0.9 constant_dynamic-update-slice_fusion
  96.6 0.7 broadcast_dynamic-update-slice_fusion.1.x_ref
  97.2 53.3 %shard_map.73 = (f32[8,272,256]{2,1,0:T(8,128)}, f32[6,272,256]{2,1,0:T(8,128)}, f32[6,272,256]{2,1,0:T(8,128)}, f32[6,272,256]{2,1,0:T(8,128)}, f32[7,272,256]{...) custom-call(f32[13,256,256]{2,1,0:T(8,128)} %broadcast_dynamic-updat, ...), custom_call_target="tpu_custom_call" | custom-call | tf_op jit(solution)/shard_map/pallas_call | solution.py:370
  150.5 0.9 slice.284
  151.4 0.9 slice.285
  152.3 0.9 slice.286
  153.2 0.9 slice.287
  154.1 151.2 %all-gather = f32[768,16,16]{2,1,0:T(8,128)} all-gather(f32[24,16,16]{2,1,0:T(8,128)S(1)} %pad_maximum_fusion.1), channel_id=2, replica_groups=mesh['gx'=8,'gy'=4] {'gx','gy'}, dimensions={0}, use_global_device_ids=true | all-gather | bytes 811008 | tf_op jit(solution)/shard_map/all_gather | solution.py:385
  305.3 6.6 %copy.19 = f32[8,4,24,16,16]{3,0,4,1,2:T(8,128)} copy(f32[8,4,24,16,16]{4,3,2,1,0:T(8,128)} %bitcast.73) | data formatting | bytes 1572864 | tf_op jit(solution)/shard_map/reshape | solution.py:386
  311.9 4.3 %reshape.11 = f32[24,128,64]{1,2,0:T(8,128)S(1)} reshape(f32[24,8,16,4,16]{2,1,4,3,0:T(8,128)} %bitcast.74) | data formatting | bytes 1572864 | tf_op jit(solution)/shard_map/reshape | solution.py:387
  316.2 0.5 copy.20
  316.7 1.3 pad.12.g_ref
  318.0 57.5 %shard_map.74 = f32[6,136,128]{2,1,0:T(8,128)} custom-call(f32[24,136,128]{2,1,0:T(8,128)} %pad.12.g_ref), custom_call_target="tpu_custom_call" | custom-call | tf_op jit(solution)/shard_map/pallas_call | solution.py:400
  375.5 1.0 pad_dynamic-slice_fusion
  376.5 0.7 pad.14.e_ref
  377.2 22.5 %shard_map.75 = f32[6,128,128]{2,1,0:T(8,128)} custom-call(f32[8,48,128]{2,1,0:T(8,128)} %pad.14.e_ref, f32[8,272,256]{2,1,0:T(8,128)} %get-tuple-element.31.refs_0_, f32[6,272,256]{2,1,0:T(8,128)} %get-tuple-element.32.refs_1_, f32[6,272,256]{2,1,0:T(8,128)} %get-tuple-element.33.refs_2_, f32[6,272,256]{2,1,0:T(8,128)} %get-tuple-element.34.refs_3_, ...), custom_call_target="tpu_custom_call" | custom-call | tf_op jit(solution)/shard_map/pallas_call | solution.py:417
  (2 shorter events, 0.0 us)
Async XLA Ops:
  51.5 11.3 %collective-permute-start = (f32[13,128,56]{1,2,0:T(8,128)S(1)}, f32[13,128,56]{1,2,0:T(8,128)S(1)}, u32[]{:S(2)}, u32[]{:S(2)}) collective-permute-start(f32[13,128,56]{1,2,0:T(8,128)S(1)} %copy.15), channel_id=1, source_target_pairs={{0,1},{1,2},{2,3},{4,5},{5,6},{6,7},{8,9},{9,10},{10,11},{12,13},{... | collective-permute-start | bytes 1118216 | tf_op jit(solution)/shard_map/ppermute | solution.py:330
  55.7 17.0 %collective-permute-start.1 = (f32[13,128,56]{1,2,0:T(8,128)S(1)}, f32[13,128,56]{1,2,0:T(8,128)S(1)}, u32[]{:S(2)}, u32[]{:S(2)}) collective-permute-start(f32[13,128,56]{1,2,0:T(8,128)S(1)} %copy.16), channel_id=1, source_target_pairs={{1,0},{2,1},{3,2},{5,4},{6,5},{7,6},{9,8},{10,9},{11,10},{13,12},{... | collective-permute-start | bytes 1118216 | tf_op jit(solution)/shard_map/ppermute | solution.py:331
  78.1 13.4 %collective-permute-start.2 = (f32[13,56,256]{2,1,0:T(8,128)}, f32[13,56,256]{2,1,0:T(8,128)}, u32[]{:S(2)}, u32[]{:S(2)}) collective-permute-start(f32[13,56,256]{2,1,0:T(8,128)} %get-tuple-element.50), channel_id=1, source_target_pairs={{0,4},{4,8},{8,12},{12,16},{16,20},{20,24},{24,28},{1,5},{5,9},{9,... | collective-permute-start | bytes 2236424 | tf_op jit(solution)/shard_map/ppermute | solution.py:330
  82.8 12.9 %collective-permute-start.3 = (f32[13,56,256]{2,1,0:T(8,128)S(1)}, f32[13,56,256]{2,1,0:T(8,128)S(1)}, u32[]{:S(2)}, u32[]{:S(2)}) collective-permute-start(f32[13,56,256]{2,1,0:T(8,128)S(1)} %get-tuple-element.49), channel_id=1, source_target_pairs={{4,0},{8,4},{12,8},{16,12},{20,16},{24,20},{28,24},{5,1},{9,5},{13... | collective-permute-start | bytes 2236424 | tf_op jit(solution)/shard_map/ppermute | solution.py:331

commit v2 on v1

--- a/solution.py
+++ b/solution.py
@@ -185,9 +185,9 @@
 
 
 def down_kernel(x_ref, lat_t, ver_t, sto_t, *refs):
-    outs, scratch = refs[: 6 * LOCAL + 4], refs[6 * LOCAL + 4 :]
+    outs, packed, scratch = refs[: 6 * LOCAL], refs[6 * LOCAL], refs[6 * LOCAL + 1 :]
     level = [outs[6 * i : 6 * i + 6] for i in range(LOCAL)]
-    coarse = outs[6 * LOCAL :]
+    coarse = scratch[5 * LOCAL :]
     own = [scratch[5 * i : 5 * i + 5] for i in range(LOCAL)]
     u, rhs = level[0][:2]
     lat, ver, sto = own[0][:3]
@@ -231,21 +231,46 @@
             cut,
             size - cut,
         )
-
-
-def coarse_kernel(g_ref, out_ref, *scratch):
+    per, h, lanes = packed.shape
+    off = FRAME >> LOCAL
+    w = lanes * per // 24
+    lane = lax.broadcasted_iota(jnp.int32, (h, lanes), 1) // w
+    for i in range(per):
+        total = jnp.zeros((h, lanes), F32)
+        for j in range(24 // per):
+            at = j * per + i
+            x = coarse[at // 6][at % 6, PAD + off : PAD + off + h, :]
+            total = jnp.where(lane == j, pltpu.roll(x, (j * w - off) % lanes, 1), total)
+        packed[i] = total
+
+
+def coarse_kernel(rows_of, g_ref, out_ref, *scratch):
     count = LEVELS - LOCAL
-    rows, columns = g_ref.shape[1:]
+    blocks, per, h, lanes = g_ref.shape
+    w = lanes * per // 24
+    columns_of = blocks // rows_of
+    rows = rows_of * h
     data = [scratch[11 * i : 11 * i + 11] for i in range(count + 1)]
     for j in range(4):
         ref = data[0][(1, 6, 7, 8)[j]]
         ref[...] = jnp.zeros_like(ref)
-
-        def take(k, carry, ref=ref, j=j):
-            ref[k, PAD : PAD + rows, :] = g_ref[6 * j + k]
-            return carry
-
-        lax.fori_loop(0, 6, take, 0)
+    lane = lax.broadcasted_iota(jnp.int32, (h, lanes), 1) // w
+
+    def take(gx, carry):
+        row = pl.multiple_of(PAD + gx * h, 8)
+        for at in range(24):
+            j, i = at // per, at % per
+            ref = data[0][(1, 6, 7, 8)[at // 6]]
+            for start in range(0, columns_of, lanes // w):
+                total = jnp.zeros((h, lanes), F32)
+                for gy in range(start, min(start + lanes // w, columns_of)):
+                    x = g_ref[gx * columns_of + gy, i]
+                    x = pltpu.roll(x, ((gy - start - j) * w) % lanes, 1)
+                    total = jnp.where(lane == gy - start, x, total)
+                ref[at % 6, pl.ds(row, h), start * w : start * w + lanes] = total
+        return carry
+
+    lax.fori_loop(0, rows_of, take, 0)
     for i in range(count):
         u, rhs, wr, wc, wv, inv, lat, ver, sto, diag, temp = data[i]
         down_level(
@@ -291,7 +316,7 @@
     u = data[0][0]
 
     def give(k, carry):
-        out_ref[k] = u[k + 1, PAD : PAD + rows, :]
+        out_ref[k] = u[k + 1, PAD : PAD + out_ref.shape[1], :]
         return carry
 
     lax.fori_loop(0, 6, give, 0)
@@ -347,7 +372,11 @@
 
 
 def on_device(field, substance, patch, planar, vertical, storage, wattage):
-    heat = jnp.repeat(jnp.repeat(lookup(patch, wattage), TILE, axis=0), TILE, axis=1)
+    small = lax.optimization_barrier(lookup(patch, wattage))
+    tall = jnp.repeat(jnp.eye(patch.shape[0], dtype=F32), TILE, axis=0)
+    flat = jnp.repeat(jnp.eye(patch.shape[1], dtype=F32), TILE, axis=1)
+    exact = functools.partial(jnp.dot, precision=lax.Precision.HIGHEST)
+    heat = exact(exact(tall, small), flat)
     x = jnp.concatenate([field, substance.astype(F32) + 1.0, heat[None]], 0)
     x = extended(extended(x, "gy", 2), "gx", 1)
     local_rows, local_cols = field.shape[1:]
@@ -366,39 +395,32 @@
     for i in range(LOCAL):
         shapes += [jax.ShapeDtypeStruct(frame(n, *dims[i]), F32) for n in (8, 6, 6, 6, 7, 6)]
         scratch += [pltpu.VMEM(frame(6, *dims[i]), F32) for _ in range(5)]
-    coarse = [jax.ShapeDtypeStruct(frame(6, *dims[LOCAL]), F32)] * 4
+    scratch += [pltpu.VMEM(frame(6, *dims[LOCAL]), F32) for _ in range(4)]
+    h, w = local_rows >> LOCAL, local_cols >> LOCAL
+    off = FRAME >> LOCAL
+    lanes = dims[LOCAL][1]
     result = pl.pallas_call(
         down_kernel,
-        out_shape=shapes + coarse,
+        out_shape=shapes + [jax.ShapeDtypeStruct((24 * w // lanes, h, lanes), F32)],
         in_specs=[vmem] + [smem] * 3,
-        out_specs=[vmem] * (6 * LOCAL + 4),
+        out_specs=[vmem] * (6 * LOCAL + 1),
         scratch_shapes=scratch,
         compiler_params=params,
     )(x, planar, vertical, storage)
-    levels, coarse = result[: 6 * LOCAL], result[6 * LOCAL :]
-    h, w = local_rows >> LOCAL, local_cols >> LOCAL
-    off = FRAME >> LOCAL
-    mine = jnp.concatenate(
-        [c[:, PAD + off : PAD + off + h, off : off + w] for c in coarse], 0
-    )
+    levels, mine = result[: 6 * LOCAL], result[6 * LOCAL]
     nx, ny = lax.axis_size("gx"), lax.axis_size("gy")
-    all_blocks = lax.all_gather(mine, ("gx", "gy"), axis=0, tiled=False)
-    all_blocks = all_blocks.reshape(nx, ny, 24, h, w).transpose(2, 0, 3, 1, 4)
-    whole = all_blocks.reshape(24, nx * h, ny * w)
+    whole = lax.all_gather(mine, ("gx", "gy"), axis=0, tiled=False)
     sizes = [
         (up_to(((nx * h) >> i) + 1, 8), up_to(((ny * w) >> i) + 1, 128))
         for i in range(LEVELS - LOCAL + 1)
     ]
-    whole = jnp.pad(
-        whole, ((0, 0), (0, sizes[0][0] - nx * h), (0, sizes[0][1] - ny * w))
-    )
     scratch = []
     for size in sizes:
         scratch += [
             pltpu.VMEM(frame(n, *size), F32) for n in (8, 6, 6, 6, 7, 6, 6, 6, 6, 6, 6)
         ]
     solved = pl.pallas_call(
-        coarse_kernel,
+        functools.partial(coarse_kernel, nx),
         out_shape=jax.ShapeDtypeStruct((6,) + sizes[0], F32),
         in_specs=[vmem],
         out_specs=vmem,

time: 402 us -> 305 us (0.76)
  blocking collectives: 151 us -> 65.8 us
  local copies, waits for them, and re-layouts: 39.3 us -> 22.9 us
    all_gather x1, blocking collectives: 151 us -> 65.8 us  [on_device(): whole = lax.all_gather(mine, ('gx', 'gy'), axis=0, tiled=False)]
    reshape x4 -> x1, local copies, waits for them, and re-layouts: 11.4 us -> 0.08 us  [on_device(): flat = jnp.repeat(jnp.eye(patch.shape[1], dtype=F32), TILE, axis=1)]
  transfers between devices with their start and end apart: 4 -> 4, of which waited for: 4 -> 4; matrix products, arithmetic and copies ran while one was open for 1% -> 2% of each run, Pallas kernels for 0% -> 0%
where the time goes in v2:
time: 305 us; the launch traced here: 299 us
  Pallas kernels  135 us (44%)
  blocking collectives  65.8 us (22%)
  other arithmetic  42.7 us (14%)
  local copies, waits for them, and re-layouts  22.9 us (8%)
  waiting for transfers between devices  21.2 us (7%)
  starting transfers between devices  11.8 us (4%)
    all_gather x1, blocking collectives, on_device(): whole = lax.all_gather(mine, ('gx', 'gy'), axis=0, tiled=False)  65.8 us
    pallas_call x1, Pallas kernels, on_device(): pl.pallas_call(functools.partial(coarse_kernel, nx), out_shape=jax.ShapeD...  58.9 us
    pallas_call x1, Pallas kernels, on_device(): pl.pallas_call(down_kernel, out_shape=shapes + [jax.ShapeDtypeStruct((24...  53.1 us
    add x1, other arithmetic, lookup(): summed = summed + jnp.where(labels == number, entries[number], 0.0)  40.6 us
    pallas_call x1, Pallas kernels, on_device(): pl.pallas_call(up_kernel, out_shape=jax.ShapeDtypeStruct(field.shape, F32...  22.5 us
    ppermute x2, waiting for transfers between devices, extended(): lax.ppermute(lax.slice_in_dim(block, size - WIDE, None, axis=dim), axis,...  11.9 us
    ppermute x2, waiting for transfers between devices, extended(): lax.ppermute(lax.slice_in_dim(block, 0, WIDE, axis=dim), axis, backward)  9.26 us
    ppermute x2, starting transfers between devices, extended(): lax.ppermute(lax.slice_in_dim(block, size - WIDE, None, axis=dim), axis,...  8.56 us
  transfers between devices with their start and end apart: 4, of which 4 were waited for; matrix products, arithmetic and copies ran while one was open for 2% of the time, Pallas kernels for 0%

profile of v2, /device:TPU:1, one launch (start us, length us, event | category | flops | bytes accessed | tf_op | source)
XLA Modules:
  0.0 299.5 jit_solution(2554822984635645136)
XLA Ops:
  0.0 2.1 fusion.3
  2.1 2.1 fusion.5
  4.1 2.1 fusion.4
  6.2 1.6 fusion.6
  7.8 40.6 %select_add_fusion = f32[8,8]{1,0:T(8,128)S(1)} fusion(s32[8,8]{1,0:T(8,128)} %param.9, f32[]{:T(128)} %bitcast.64, f32[]{:T(128)} %bitcast.63, f32[]{:T(128)} %bitcast.62, f32[]{:T(128)} %bitcast.61, f32[]{:T(128)} %bitcast.60, f32[]{:T(128)} %bitcast.59, f32[]{:T(128)} %bitcast.58, f32[]{:T(128)} %bitcast.57, f32[]{:T(128)} %bitcast.56, f32[]{:T(128)} %bitcast.55, ...), kind=kLoop, calls=%fused_computation.9 | loop fusion | flops 12224 | bytes 768 | tf_op jit(solution)/shard_map/add | solution.py:366
  48.4 0.1 broadcast_in_dim.343
  48.5 0.1 reshape.7
  48.6 1.0 convert_add_fusion
  49.6 0.2 fusion.7
  49.8 0.2 convolution_bitcast_fusion
  50.0 1.1 pad_maximum_fusion
  51.1 0.3 fusion.2
  51.4 0.3 copy.10
  51.7 4.0 %collective-permute-start = (f32[13,128,56]{1,2,0:T(8,128)S(1)}, f32[13,128,56]{1,2,0:T(8,128)S(1)}, u32[]{:S(2)}, u32[]{:S(2)}) collective-permute-start(f32[13,128,56]{1,2,0:T(8,128)S(1)} %copy.10), channel_id=1, source_target_pairs={{0,1},{1,2},{2,3},{4,5},{5,6},{6,7},{8,9},{9,10},{10,11},{12,13},{... | collective-permute-start | bytes 1118216 | tf_op jit(solution)/shard_map/ppermute | solution.py:355
  55.6 0.3 copy.11
  55.9 1.3 collective-permute-start.1
  57.2 5.7 %collective-permute-done = f32[13,128,56]{1,2,0:T(8,128)S(1)} collective-permute-done((f32[13,128,56]{1,2,0:T(8,128)S(1)}, f32[13,128,56]{1,2,0:T(8,128)S(1)}, u32[]{:S(2)}, u32[]{:S(2)}) %collective-permute-start) | collective-permute-done | bytes 372768 | tf_op jit(solution)/shard_map/ppermute | solution.py:355
  63.0 1.2 copy.12
  64.2 8.7 %collective-permute-done.1 = f32[13,128,56]{1,2,0:T(8,128)S(1)} collective-permute-done((f32[13,128,56]{1,2,0:T(8,128)S(1)}, f32[13,128,56]{1,2,0:T(8,128)S(1)}, u32[]{:S(2)}, u32[]{:S(2)}) %collective-permute-start.1) | collective-permute-done | bytes 372768 | tf_op jit(solution)/shard_map/ppermute | solution.py:356
  72.9 1.2 copy.13
  74.1 0.1 broadcast_in_dim.276
  74.2 3.1 %concatenate.10 = f32[13,128,256]{2,1,0:T(8,128)S(1)} concatenate(f32[13,128,8]{2,1,0:T(8,128)S(1)} %broadcast_in_dim.276, f32[13,128,56]{2,1,0:T(8,128)} %copy.12, f32[13,128,128]{2,1,0:T(8,128)S(1)} %pad_maximum_fusion, f32[13,128,56]{2,1,0:T(8,128)} %copy.13, f32[13,128,8]{2,1,0:T(8,128)S(1)} %broadcast_in_dim.276), dimensions={2} | concatenate | bytes 3407872 | tf_op jit(solution)/shard_map/concatenate | solution.py:360
  77.3 1.0 fusion.1
  78.4 4.6 %collective-permute-start.2 = (f32[13,56,256]{2,1,0:T(8,128)}, f32[13,56,256]{2,1,0:T(8,128)}, u32[]{:S(2)}, u32[]{:S(2)}) collective-permute-start(f32[13,56,256]{2,1,0:T(8,128)} %get-tuple-element.44), channel_id=1, source_target_pairs={{0,4},{4,8},{8,12},{12,16},{16,20},{20,24},{24,28},{1,5},{5,9},{9,... | collective-permute-start | bytes 2236424 | tf_op jit(solution)/shard_map/ppermute | solution.py:355
  83.0 1.9 collective-permute-start.3
  84.9 0.7 broadcast_dynamic-update-slice_fusion
  85.6 6.2 %collective-permute-done.2 = f32[13,56,256]{2,1,0:T(8,128)} collective-permute-done((f32[13,56,256]{2,1,0:T(8,128)}, f32[13,56,256]{2,1,0:T(8,128)}, u32[]{:S(2)}, u32[]{:S(2)}) %collective-permute-start.2) | collective-permute-done | bytes 745504 | tf_op jit(solution)/shard_map/ppermute | solution.py:355
  91.8 2.1 constant_dynamic-update-slice_fusion.2
  93.9 1.4 constant_dynamic-update-slice_fusion.1
  95.3 0.6 collective-permute-done.3
  95.8 0.9 constant_dynamic-update-slice_fusion
  96.8 0.7 broadcast_dynamic-update-slice_fusion.1.x_ref
  97.4 53.1 %shard_map.73 = (f32[8,272,256]{2,1,0:T(8,128)}, f32[6,272,256]{2,1,0:T(8,128)}, f32[6,272,256]{2,1,0:T(8,128)}, f32[6,272,256]{2,1,0:T(8,128)}, f32[7,272,256]{...) custom-call(f32[13,256,256]{2,1,0:T(8,128)} %broadcast_dynamic-updat, ...), custom_call_target="tpu_custom_call" | custom-call | tf_op jit(solution)/shard_map/pallas_call | solution.py:402
  150.6 65.8 %all-gather = f32[96,16,128]{2,1,0:T(8,128)} all-gather(f32[3,16,128]{2,1,0:T(8,128)} %get-tuple-element.24), channel_id=2, replica_groups=mesh['gx'=8,'gy'=4] {'gx','gy'}, dimensions={0}, use_global_device_ids=true | all-gather | bytes 811008 | tf_op jit(solution)/shard_map/all_gather | solution.py:412
  216.4 58.9 %shard_map.74 = f32[6,136,128]{2,1,0:T(8,128)} custom-call(f32[32,3,16,128]{3,2,1,0:T(8,128)} %bitcast.72), custom_call_target="tpu_custom_call" | custom-call | tf_op jit(solution)/shard_map/pallas_call | solution.py:422
  275.3 1.0 pad_dynamic-slice_fusion
  276.3 0.7 pad.9.e_ref
  277.0 22.5 %shard_map.75 = f32[6,128,128]{2,1,0:T(8,128)} custom-call(f32[8,48,128]{2,1,0:T(8,128)} %pad.9.e_ref, f32[8,272,256]{2,1,0:T(8,128)} %get-tuple-element.25.refs_0_, f32[6,272,256]{2,1,0:T(8,128)} %get-tuple-element.26.refs_1_, f32[6,272,256]{2,1,0:T(8,128)} %get-tuple-element.27.refs_2_, f32[6,272,256]{2,1,0:T(8,128)} %get-tuple-element.28.refs_3_, ...), custom_call_target="tpu_custom_call" | custom-call | tf_op jit(solution)/shard_map/pallas_call | solution.py:439
  (2 shorter events, 0.0 us)
Async XLA Ops:
  51.7 11.3 %collective-permute-start = (f32[13,128,56]{1,2,0:T(8,128)S(1)}, f32[13,128,56]{1,2,0:T(8,128)S(1)}, u32[]{:S(2)}, u32[]{:S(2)}) collective-permute-start(f32[13,128,56]{1,2,0:T(8,128)S(1)} %copy.10), channel_id=1, source_target_pairs={{0,1},{1,2},{2,3},{4,5},{5,6},{6,7},{8,9},{9,10},{10,11},{12,13},{... | collective-permute-start | bytes 1118216 | tf_op jit(solution)/shard_map/ppermute | solution.py:355
  55.9 17.0 %collective-permute-start.1 = (f32[13,128,56]{1,2,0:T(8,128)S(1)}, f32[13,128,56]{1,2,0:T(8,128)S(1)}, u32[]{:S(2)}, u32[]{:S(2)}) collective-permute-start(f32[13,128,56]{1,2,0:T(8,128)S(1)} %copy.11), channel_id=1, source_target_pairs={{1,0},{2,1},{3,2},{5,4},{6,5},{7,6},{9,8},{10,9},{11,10},{13,12},{... | collective-permute-start | bytes 1118216 | tf_op jit(solution)/shard_map/ppermute | solution.py:356
  78.4 13.4 %collective-permute-start.2 = (f32[13,56,256]{2,1,0:T(8,128)}, f32[13,56,256]{2,1,0:T(8,128)}, u32[]{:S(2)}, u32[]{:S(2)}) collective-permute-start(f32[13,56,256]{2,1,0:T(8,128)} %get-tuple-element.44), channel_id=1, source_target_pairs={{0,4},{4,8},{8,12},{12,16},{16,20},{20,24},{24,28},{1,5},{5,9},{9,... | collective-permute-start | bytes 2236424 | tf_op jit(solution)/shard_map/ppermute | solution.py:355
  83.0 12.9 %collective-permute-start.3 = (f32[13,56,256]{2,1,0:T(8,128)S(1)}, f32[13,56,256]{2,1,0:T(8,128)S(1)}, u32[]{:S(2)}, u32[]{:S(2)}) collective-permute-start(f32[13,56,256]{2,1,0:T(8,128)S(1)} %get-tuple-element.43), channel_id=1, source_target_pairs={{4,0},{8,4},{12,8},{16,12},{20,16},{24,20},{28,24},{5,1},{9,5},{13... | collective-permute-start | bytes 2236424 | tf_op jit(solution)/shard_map/ppermute | solution.py:356
